TPU v7x, 256 devices: a whole 4x4x8 slice. The times are simulated.
256 devices in a mesh: seq: 16 (over y, x), grp: 16 (over z, core).
Axes of the slice: x: 4, y: 4, z: 8, core: 2. Of those that a mesh axis runs over, the one named last changes fastest.
Arguments:
- actions: int32 [32, 7], P('grp'), may hold values from 0 to 255
- lengths: int32 [32], P('grp'), may hold values from 2048 to 4096
- embed: bfloat16 [256, 4096], replicated, may hold values from -6 to 6
- attn_gain: float32 [4096], replicated, may hold values from 0.1 to 1.9
- w_query: bfloat16 [4096, 4096], P('grp', 'seq'), may hold values from -0.09375 to 0.09375
- w_key: bfloat16 [4096, 4096], P('grp', 'seq'), may hold values from -0.140625 to 0.140625
- w_value: bfloat16 [4096, 4096], P('grp', 'seq'), may hold values from -0.09375 to 0.09375
- w_out: bfloat16 [4096, 4096], P('grp', 'seq'), may hold values from -0.09375 to 0.09375
- key_cache: bfloat16 [32, 4096, 4096], P('grp', 'seq'), may hold values from -136 to 136
- value_cache: bfloat16 [32, 4096, 4096], P('grp', 'seq'), may hold values from -6 to 6
- final_gain: float32 [4096], replicated, may hold values from 0.1 to 1.9
- head: bfloat16 [256, 4096], P('seq'), may hold values from -0.25 to 0.25
Outputs:
- logprob: float32 [32, 7, 256], P('grp', None, 'seq')
Inputs may be any that keep to these rules, and one draw needn't show every extreme that they name: Robot r's prompt occupies cache positions 0 to lengths[r] - 1.
All inputs are finite; a program needn't handle non-finite values.
Results may differ from a plain program's by a relative error of at most 0.008.
Values may be sent and summed in bfloat16 or wider, within the bound.
No kernel may reach another device: no remote copies, remote signals or barrier semaphores. Data moves between devices by JAX's collectives and lax.ppermute only.
A program may use at most 64 MiB of HBM per device.

v0:
```python
import jax
import jax.numpy as jnp
from jax import lax
from jax.sharding import Mesh
from jax.sharding import PartitionSpec as P

HEAD_DIM = 128
SEQ = ("seq_0", "seq_1")


def split_up(shard, dim, devices):
    before, after = (shard.shape[:dim], shard.shape[dim + 1 :])
    return jnp.moveaxis(shard.reshape(*before, devices, -1, *after), dim, 0)


def sum_at_owner(shard, axis, dim):
    pieces = split_up(shard, dim, lax.axis_size(axis))
    arrived = lax.all_to_all(pieces, axis, split_axis=0, concat_axis=0, tiled=True)
    return arrived.sum(axis=0)


def sent_together(arrays, axis, dim, along):
    widths = [a.shape[along] for a in arrays]
    both = jnp.concatenate(arrays, axis=along)
    out = lax.all_gather(both, axis, axis=dim, tiled=True)
    return tuple(jnp.split(out, [sum(widths[:k]) for k in range(1, len(widths))], axis=along))


def all_in_one(shard, axis):
    leaves = jax.tree.leaves(shard)
    order = sorted(range(len(leaves)), key=lambda k: -leaves[k].size)
    width = (1, *leaves[order[0]].shape)[-1]
    lines = [
        jnp.pad(leaves[k].reshape(-1), (0, -leaves[k].size % width)).reshape(-1, width)
        for k in order
    ]
    both, at, found = (lax.all_gather(jnp.concatenate(lines), axis), 0, {})
    for k, line in zip(order, lines):
        share = both[:, at : at + len(line)].reshape(len(both), -1)
        found[k] = share[:, : leaves[k].size].reshape(-1, *leaves[k].shape)
        at += len(line)
    numbers = iter(range(len(leaves)))
    return jax.tree.map(lambda _: found[next(numbers)], shard)


def merged_by_axis(shard, axes, combine):
    for axis in axes:
        pieces = all_in_one(shard, axis)
        shard = jax.tree.map(lambda part: part[0], pieces)
        for k in range(1, lax.axis_size(axis)):
            shard = combine(shard, jax.tree.map(lambda part: part[k], pieces))
    return shard


def sum_at_owner_2(shard, axis, dim):
    devices = lax.axis_size(axis)
    pieces = lax.all_to_all(split_up(shard, dim, devices), axis, 0, 0, tiled=True)
    return jnp.sum(pieces.astype(jnp.float32), axis=0)


def joined_along(pieces, dim):
    pieces = jnp.moveaxis(pieces, 0, dim)
    lengths = pieces.shape
    return pieces.reshape(*lengths[:dim], lengths[dim] * lengths[dim + 1], *lengths[dim + 2 :])


def copy_for_each(shard, axis):
    devices = lax.axis_size(axis)
    return lax.all_to_all(
        jnp.broadcast_to(shard[None], (devices, *shard.shape)), axis, 0, 0, tiled=True
    )


def collect(shard, axis, dim):
    return joined_along(copy_for_each(shard, axis), dim)


def gathered_once(shard, axis):
    leaves = jax.tree.leaves(shard)
    order = sorted(range(len(leaves)), key=lambda k: -leaves[k].size)
    width = (1, *leaves[order[0]].shape)[-1]
    lines = [
        jnp.pad(leaves[k].reshape(-1), (0, -leaves[k].size % width)).reshape(-1, width)
        for k in order
    ]
    both, at, found = (copy_for_each(jnp.concatenate(lines), axis), 0, {})
    for k, line in zip(order, lines):
        share = both[:, at : at + len(line)].reshape(len(both), -1)
        found[k] = share[:, : leaves[k].size].reshape(-1, *leaves[k].shape)
        at += len(line)
    numbers = iter(range(len(leaves)))
    return jax.tree.map(lambda _: found[next(numbers)], shard)


def combined_pairwise(pieces, combine):
    while len(jax.tree.leaves(pieces)[0]) > 1:
        pieces = jax.vmap(combine)(
            *(jax.tree.map(lambda part: part[side::2], pieces) for side in (0, 1))
        )
    return jax.tree.map(lambda part: part[0], pieces)


def combined_all(shard, axis, combine):
    pieces = gathered_once(shard, axis)
    return combined_pairwise(pieces, combine)


def rms_scale(values, gain):
    mean_square = jnp.mean(values * values, axis=-1, keepdims=True)
    return values * lax.rsqrt(mean_square + 1e-05) * gain


def rotate(values, places):
    half = values.shape[-1] // 2
    freq = 10000.0 ** (-(jnp.arange(half, dtype=jnp.float32) * 2.0 / values.shape[-1]))
    angle = places[..., None, None] * freq
    first = values[..., :half]
    second = values[..., half:]
    cosine = jnp.cos(angle)
    sine = jnp.sin(angle)
    return jnp.concatenate(
        [first * cosine - second * sine, second * cosine + first * sine], axis=-1
    )


def join_softmax(left, right):
    top = jnp.maximum(left[0], right[0])
    left_factor = jnp.exp(left[0] - top)
    right_factor = jnp.exp(right[0] - top)
    total = left[1] * left_factor + right[1] * right_factor
    acc = left[2] * left_factor[..., None] + right[2] * right_factor[..., None]
    return (top, total, acc)


def join_totals(left, right):
    top = jnp.maximum(left[0], right[0])
    return (top, left[1] * jnp.exp(left[0] - top) + right[1] * jnp.exp(right[0] - top))


def on_device(
    actions,
    lengths,
    embed,
    attn_gain,
    w_query,
    w_key,
    w_value,
    w_out,
    key_cache,
    value_cache,
    final_gain,
    head,
):
    seq_index = lax.axis_index(SEQ)
    seq_count = lax.axis_size(SEQ)
    robots, steps = actions.shape
    prompt_dev = key_cache.shape[1]
    width = key_cache.shape[2]
    col_block = w_query.shape[1]
    head_dim = HEAD_DIM
    heads = width // head_dim
    local_heads = col_block // head_dim
    scale = head_dim ** (-0.5)
    bins = jnp.arange(embed.shape[0], dtype=jnp.int32)
    onehot = (actions[:, :, None] == bins[None, None, :]).astype(jnp.bfloat16)
    inputs = jnp.einsum("rtb,bd->rtd", onehot, embed, preferred_element_type=jnp.float32)
    normed = rms_scale(inputs, attn_gain).astype(jnp.bfloat16)
    places = (lengths[:, None] + jnp.arange(steps, dtype=jnp.int32)[None, :]).astype(jnp.float32)
    prompt_places = seq_index * prompt_dev + jnp.arange(prompt_dev, dtype=jnp.int32)
    prompt_valid = prompt_places[None, :] < lengths[:, None]
    cache_keys = key_cache.reshape(robots, prompt_dev, heads, head_dim)
    cache_values = value_cache.reshape(robots, prompt_dev, heads, head_dim)
    empty = jnp.zeros((robots, 0, heads, head_dim), jnp.bfloat16)
    window_keys = empty
    window_values = empty
    rows = robots * steps
    block_norm = normed.reshape(rows, width)
    spread_rows = lax.all_to_all(block_norm, "grp", split_axis=1, concat_axis=0, tiled=True)
    terms = jnp.concatenate(
        [
            jnp.dot(spread_rows, w_query, preferred_element_type=jnp.float32),
            jnp.dot(spread_rows, w_key, preferred_element_type=jnp.float32),
            jnp.dot(spread_rows, w_value, preferred_element_type=jnp.float32),
        ],
        axis=1,
    )
    sums = sum_at_owner(terms, "grp", 0)

    def heads_of(flat):
        return flat.reshape(robots, steps, local_heads, head_dim)

    query = (
        rotate(heads_of(sums[:, :col_block]), places).astype(jnp.bfloat16).reshape(rows, col_block)
    )
    key = (
        rotate(heads_of(sums[:, col_block : 2 * col_block]), places)
        .astype(jnp.bfloat16)
        .reshape(rows, col_block)
    )
    value = sums[:, 2 * col_block :].astype(jnp.bfloat16)
    query, key, value = sent_together((query, key, value), SEQ, 1, 0)
    query = query.reshape(robots, steps, heads, head_dim)
    window_keys = jnp.concatenate(
        [window_keys, key.reshape(robots, steps, heads, head_dim)], axis=1
    )
    window_values = jnp.concatenate(
        [window_values, value.reshape(robots, steps, heads, head_dim)], axis=1
    )
    seen = 0 + steps
    window_index = jnp.arange(seen, dtype=jnp.int32)
    step_index = 0 + jnp.arange(steps, dtype=jnp.int32)
    window_valid = (window_index[None, :] <= step_index[:, None]) & (
        window_index % seq_count == seq_index
    )[None, :]
    prompt_mask = prompt_valid[:, None, None, :]
    window_mask = window_valid[None, :, None, :]
    prompt_scores = (
        jnp.einsum("rthd,rphd->rthp", query, cache_keys, preferred_element_type=jnp.float32) * scale
    )
    window_scores = (
        jnp.einsum("rthd,rjhd->rthj", query, window_keys, preferred_element_type=jnp.float32)
        * scale
    )
    prompt_scores = jnp.where(prompt_mask, prompt_scores, -1e30)
    window_scores = jnp.where(window_mask, window_scores, -1e30)
    local_max = jnp.maximum(jnp.max(prompt_scores, axis=-1), jnp.max(window_scores, axis=-1))
    prompt_e = jnp.where(prompt_mask, jnp.exp(prompt_scores - local_max[..., None]), 0.0)
    window_e = jnp.where(window_mask, jnp.exp(window_scores - local_max[..., None]), 0.0)
    total = jnp.sum(prompt_e, axis=-1) + jnp.sum(window_e, axis=-1)
    acc = jnp.einsum(
        "rthp,rphd->rthd",
        prompt_e.astype(jnp.bfloat16),
        cache_values,
        preferred_element_type=jnp.float32,
    )
    acc = acc + jnp.einsum(
        "rthj,rjhd->rthd",
        window_e.astype(jnp.bfloat16),
        window_values,
        preferred_element_type=jnp.float32,
    )
    total, acc = (total, acc)
    top, total, acc = merged_by_axis((local_max, total, acc), SEQ, join_softmax)
    attended = (acc / total[..., None]).astype(jnp.bfloat16).reshape(rows, width)
    spread_attended = lax.all_to_all(attended, "grp", split_axis=1, concat_axis=0, tiled=True)
    out_terms = jnp.dot(spread_attended, w_out, preferred_element_type=jnp.float32)
    out_part = sum_at_owner_2(out_terms.astype(jnp.bfloat16), "grp", 0)
    branch = collect(out_part, SEQ, 1)
    residual = inputs.reshape(rows, width) + branch
    final = rms_scale(residual, final_gain).astype(jnp.bfloat16)
    logits = lax.dot_general(
        final, head, (((1,), (1,)), ((), ())), preferred_element_type=jnp.float32
    )
    row_max = jnp.max(logits, axis=-1)
    local_total = jnp.sum(jnp.exp(logits - row_max[:, None]), axis=-1)
    top_logit, exp_total = combined_all((row_max, local_total), SEQ, join_totals)
    logprob = logits - top_logit[:, None] - jnp.log(exp_total)[:, None]
    result = logprob.reshape(robots, steps, logits.shape[1])
    return result


def solution(mesh):
    torus = Mesh(mesh.devices.reshape(4, 4, mesh.shape["grp"]), ("seq_0", "seq_1", "grp"))
    in_specs = (
        P("grp", None),
        P("grp"),
        P(),
        P(),
        P("grp", SEQ),
        P("grp", SEQ),
        P("grp", SEQ),
        P("grp", SEQ),
        P("grp", SEQ, None),
        P("grp", SEQ, None),
        P(),
        P(SEQ, None),
    )
    out_specs = P("grp", None, SEQ)
    return jax.shard_map(
        on_device, mesh=torus, in_specs=in_specs, out_specs=out_specs, check_vma=False
    )
```

profile of v0, /device:TPU:1, one launch (start us, length us, event | category | flops | bytes accessed | tf_op | source)
XLA Modules:
  0.0 184.5 jit_solution(1616942880006318692)
XLA Ops:
  0.0 1.6 copy-done
  1.6 1.2 multiply_reduce_fusion.1
  2.8 0.8 multiply_convert_fusion.1
  3.6 0.2 all_to_all.38
  3.8 18.6 %all_to_all.55 = bf16[14,16,256]{2,0,1:T(8,128)(2,1)S(1)} all-to-all(bf16[14,16,256]{2,0,1:T(8,128)(2,1)S(1)} %copy.58), channel_id=1, replica_groups=mesh['seq_0'=4,'seq_1'=4,'grp'=16] {'grp'}, dimensions={1} | all-to-all | bytes 229376 | tf_op jit(solution)/shard_map/all_to_all | solution.py:178
  22.5 1.1 fusion.65
  23.6 0.2 fusion.66
  23.8 0.2 fusion.67
  24.1 1.0 reshape.569
  25.0 4.2 %all-to-all-start.1 = ((f32[16,14,768]{2,1,0:T(8,128)}), f32[16,14,768]{2,1,0:T(8,128)}, u32[]{:S(2)}, u32[]{:S(2)}) async-start(f32[16,14,768]{2,1,0:T(8,128)} %reshape.569), calls=%async_computation.1 | async-start | bytes 1572864 | tf_op jit(solution)/shard_map/all_to_all | solution.py:18
  29.4 0.1 multiply_cosine_fusion
  29.6 22.2 %all-to-all-done.1 = f32[16,14,768]{2,1,0:T(8,128)} async-done(((f32[16,14,768]{2,1,0:T(8,128)}), f32[16,14,768]{2,1,0:T(8,128)}, u32[]{:S(2)}, u32[]{:S(2)}) %all-to-all-start.1) | async-done | bytes 688160 | tf_op jit(solution)/shard_map/all_to_all | solution.py:18
  51.8 1.2 reduce_sum.64
  53.1 0.1 subtract_convert_fusion.1
  53.2 0.1 pad_maximum_fusion.4
  53.3 0.1 pad_maximum_fusion.5
  53.4 19.9 %all_gather.15 = bf16[42,4096]{1,0:T(8,128)(2,1)S(1)} all-gather(bf16[42,256]{1,0:T(8,128)(2,1)S(1)} %pad_maximum_fusion.3), channel_id=1, replica_groups=mesh['seq_0'=4,'seq_1'=4,'grp'=16] {'seq_0','seq_1'}, dimensions={1}, use_global_device_ids=true | all-gather | bytes 365568 | tf_op jit(solution)/shard_map/all_gather | solution.py:25
  73.5 0.2 convolution_multiply_fusion
  73.7 0.2 copy.93
  73.8 0.1 fusion.45
  74.0 0.1 copy.78
  74.1 3.5 %fusion.63 = (f32[2,7,32]{1,2,0:T(8,128)S(1)}, f32[2,7,32,256]{3,1,2,0:T(8,128)S(1)}) fusion(bf16[2,7,32,128]{3,2,1,0:T(8,128)(2,1)S(1)} %bitcast.185, pred[2,256]{1,0:T(4,128)(4,1)S(1)} %broadcast_compare_fusion, bf16[2,256,4096]{2,1,0:T(8,128)(2,1)} %param.20), kind=kOutput, calls=%fused_computation.130 | convolution fusion | flops 29703744 | bytes 4770048 | tf_op jit(solution)/shard_map/rthd,rphd->rthp/dot_general | solution.py:218
  77.6 0.1 copy.66
  77.7 0.1 copy.70
  77.7 0.2 fusion.53
  77.9 0.2 copy.68
  78.1 0.3 fusion.23
  78.4 0.2 convolution_bitcast_fusion
  78.6 2.9 %fusion.20 = f32[2,7,32,128]{3,1,2,0:T(8,128)S(1)} fusion(f32[2,7,32,128]{3,1,2,0:T(8,128)S(1)} %convolution_bitcast_fusion, f32[2,7,32,256]{3,1,2,0:T(8,128)S(1)} %get-tuple-element.74, f32[2,7,32]{1,2,0:T(8,128)S(1)} %max.134, pred[2,256]{1,0:T(4,128)(4,1)S(1)} %broadcast_compare_fusion, bf16[2,256,4096]{2,1,0:T(8,128)(2,1)} %param.21), kind=kOutput, calls=%fused_computation.12 | convolution fusion | flops 29761536 | bytes 5114112 | tf_op jit(solution)/shard_map/rthp,rphd->rthd/dot_general | solution.py:230
  81.6 0.1 copy.79
  81.7 0.1 copy.72
  81.8 0.1 add.171
  82.0 10.7 %all-gather = f32[1824,128]{1,0:T(8,128)S(1)} all-gather(f32[456,128]{1,0:T(8,128)S(1)} %pad_maximum_fusion.1), channel_id=2, replica_groups=mesh['seq_0'=4,'seq_1'=4,'grp'=16] {'seq_0'}, dimensions={0}, use_global_device_ids=true | all-gather | bytes 1167360 | tf_op jit(solution)/shard_map/all_gather | solution.py:37
  92.8 0.4 fusion.30
  93.2 11.3 %all-gather.1 = f32[1824,128]{1,0:T(8,128)S(1)} all-gather(f32[456,128]{1,0:T(8,128)S(1)} %pad_maximum_fusion.2), channel_id=3, replica_groups=mesh['seq_0'=4,'seq_1'=4,'grp'=16] {'seq_1'}, dimensions={0}, use_global_device_ids=true | all-gather | bytes 1167360 | tf_op jit(solution)/shard_map/all_gather | solution.py:37
  105.7 0.8 div.27
  106.5 1.0 div.28
  107.5 0.8 mul.403
  108.3 1.7 mul.404
  110.0 0.8 mul.406
  110.8 1.7 mul.407
  112.5 0.8 mul.409
  113.3 1.7 mul.410
  115.0 0.8 mul.412
  115.8 1.7 mul.413
  117.5 0.8 mul.415
  118.3 1.7 mul.416
  120.0 0.8 mul.418
  120.8 1.7 mul.419
  122.5 1.7 divide_convert_fusion
  124.3 21.9 %all_to_all.56 = bf16[14,16,256]{2,0,1:T(8,128)(2,1)S(1)} all-to-all(bf16[14,16,256]{2,0,1:T(8,128)(2,1)S(1)} %copy.73), channel_id=1, replica_groups=mesh['seq_0'=4,'seq_1'=4,'grp'=16] {'grp'}, dimensions={1} | all-to-all | bytes 229376 | tf_op jit(solution)/shard_map/all_to_all | solution.py:245
  146.2 1.1 convolution_convert_fusion
  147.3 11.6 %all_to_all.57 = bf16[16,14,256]{2,1,0:T(8,128)(2,1)S(1)} all-to-all(bf16[16,14,256]{2,1,0:T(8,128)(2,1)S(1)} %reshape.586), channel_id=1, replica_groups=mesh['seq_0'=4,'seq_1'=4,'grp'=16] {'grp'}, dimensions={0} | all-to-all | bytes 229376 | tf_op jit(solution)/shard_map/all_to_all | solution.py:57
  158.9 0.7 broadcast_in_dim.49
  159.6 4.9 %all-to-all-start.4 = ((f32[16,14,256]{2,1,0:T(8,128)}), f32[16,14,256]{2,1,0:T(8,128)S(1)}, u32[]{:S(2)}, u32[]{:S(2)}) async-start(f32[16,14,256]{2,1,0:T(8,128)} %broadcast_in_dim.49), calls=%async_computation.4 | async-start | bytes 524288 | tf_op jit(solution)/shard_map/all_to_all | solution.py:69
  164.5 8.5 %all-to-all-done.4 = f32[16,14,256]{2,1,0:T(8,128)S(1)} async-done(((f32[16,14,256]{2,1,0:T(8,128)}), f32[16,14,256]{2,1,0:T(8,128)S(1)}, u32[]{:S(2)}, u32[]{:S(2)}) %all-to-all-start.4) | async-done | bytes 229408 | tf_op jit(solution)/shard_map/all_to_all | solution.py:69
  173.0 0.1 copy.74
  173.3 0.1 multiply_reduce_fusion
  173.4 0.1 rsqrt.21
  173.5 0.2 copy.92
  173.7 0.4 fusion.64
  174.0 0.2 exponential_reduce_fusion
  174.3 9.2 %all_to_all.58 = f32[16,2,14]{2,1,0:T(2,128)S(1)} all-to-all(f32[16,2,14]{2,1,0:T(2,128)S(1)} %broadcast_in_dim.50), channel_id=1, replica_groups=mesh['seq_0'=4,'seq_1'=4,'grp'=16] {'seq_0','seq_1'}, dimensions={0} | all-to-all | bytes 3584 | tf_op jit(solution)/shard_map/all_to_all | solution.py:69
  183.9 0.6 copy.77
  (101 shorter events, 2.5 us)
Async XLA Ops:
  0.0 1.6 copy-start
  0.0 23.6 %copy-start.1 = (bf16[256,256]{1,0:T(8,128)(2,1)S(1)}, bf16[256,256]{1,0:T(8,128)(2,1)}, u32[]{:S(2)}) copy-start(bf16[256,256]{1,0:T(8,128)(2,1)} %param.17) | copy-start | bytes 393220
  0.0 23.8 %copy-start.2 = (bf16[256,256]{1,0:T(8,128)(2,1)S(1)}, bf16[256,256]{1,0:T(8,128)(2,1)}, u32[]{:S(2)}) copy-start(bf16[256,256]{1,0:T(8,128)(2,1)} %param.18) | copy-start | bytes 393220
  2.8 26.5 %copy-start.5 = (s32[2]{0:T(128)S(1)}, s32[2]{0:T(128)}, u32[]{:S(2)}) copy-start(s32[2]{0:T(128)} %param.13) | copy-start | bytes 28
  25.0 26.8 %all-to-all-start.1 = ((f32[16,14,768]{2,1,0:T(8,128)}), f32[16,14,768]{2,1,0:T(8,128)}, u32[]{:S(2)}, u32[]{:S(2)}) async-start(f32[16,14,768]{2,1,0:T(8,128)} %reshape.569), calls=%async_computation.1 | async-start | bytes 1572864 | tf_op jit(solution)/shard_map/all_to_all | solution.py:18
  122.5 51.1 %copy-start.4 = (f32[4096]{0:T(1024)S(1)}, f32[4096]{0:T(1024)}, u32[]{:S(2)}) copy-start(f32[4096]{0:T(1024)} %param.22) | copy-start | bytes 49156
  124.2 49.5 %copy-start.3 = (bf16[16,4096]{1,0:T(8,128)(2,1)S(1)}, bf16[16,4096]{1,0:T(8,128)(2,1)}, u32[]{:S(2)}) copy-start(bf16[16,4096]{1,0:T(8,128)(2,1)} %param.23) | copy-start | bytes 393220
  159.6 13.4 %all-to-all-start.4 = ((f32[16,14,256]{2,1,0:T(8,128)}), f32[16,14,256]{2,1,0:T(8,128)S(1)}, u32[]{:S(2)}, u32[]{:S(2)}) async-start(f32[16,14,256]{2,1,0:T(8,128)} %broadcast_in_dim.49), calls=%async_computation.4 | async-start | bytes 524288 | tf_op jit(solution)/shard_map/all_to_all | solution.py:69
where the time goes:
time: 185 us
  blocking collectives  103 us (56%)
  waiting for transfers between devices  30.7 us (17%)
  local copies, waits for them, and re-layouts  24.2 us (13%)
  matrix products  10.8 us (6%)
  starting transfers between devices  9.04 us (5%)
  other arithmetic  5.88 us (3%)
    all_to_all x1, waiting for transfers between devices, sum_at_owner(): lax.all_to_all(pieces, axis, split_axis=0, concat_axis=0, tiled=True)  22.2 us
    all_gather x2, blocking collectives, all_in_one(): both, at, found = (lax.all_gather(jnp.concatenate(lines), axis), 0, {})  22.1 us
    all_to_all x1, blocking collectives, on_device(): lax.all_to_all(attended, 'grp', split_axis=1, concat_axis=0, tiled=True)  21.9 us
    all_gather x1, blocking collectives, sent_together(): out = lax.all_gather(both, axis, axis=dim, tiled=True)  19.9 us
    all_to_all x1, blocking collectives, on_device(): lax.all_to_all(block_norm, 'grp', split_axis=1, concat_axis=0, tiled=True)  18.6 us
    mul x12, local copies, waits for them, and re-layouts, join_softmax(): acc = left[2] * left_factor[..., None] + right[2] * right_factor[..., None]  15 us
    all_to_all x1, blocking collectives, sum_at_owner_2(): lax.all_to_all(split_up(shard, dim, devices), axis, 0, 0, tiled=True)  11.6 us
    all_to_all x1, blocking collectives, copy_for_each(): lax.all_to_all(jnp.broadcast_to(shard[None], (devices, *shard.shape)), ax...  9.25 us
  transfers between devices with their start and end apart: 2, of which 2 were waited for; matrix products, arithmetic and copies ran while one was open for 0% of the time, Pallas kernels for 0%

commit v1 on v0

--- a/solution.py
+++ b/solution.py
@@ -3,6 +3,7 @@
 from jax import lax
 from jax.sharding import Mesh
 from jax.sharding import PartitionSpec as P
+from jax.lax import all_to_all, axis_size
 
 HEAD_DIM = 128
 SEQ = ("seq_0", "seq_1")
@@ -242,7 +243,15 @@
     total, acc = (total, acc)
     top, total, acc = merged_by_axis((local_max, total, acc), SEQ, join_softmax)
     attended = (acc / total[..., None]).astype(jnp.bfloat16).reshape(rows, width)
-    spread_attended = lax.all_to_all(attended, "grp", split_axis=1, concat_axis=0, tiled=True)
+    spread_attended = jnp.concatenate(
+        all_to_all(
+            jnp.stack(jnp.split(attended, axis_size("grp"), 1), 0),
+            axis_name="grp",
+            split_axis=0,
+            concat_axis=0,
+        ),
+        0,
+    )
     out_terms = jnp.dot(spread_attended, w_out, preferred_element_type=jnp.float32)
     out_part = sum_at_owner_2(out_terms.astype(jnp.bfloat16), "grp", 0)
     branch = collect(out_part, SEQ, 1)

time: 185 us -> 171 us (0.924)
  local copies, waits for them, and re-layouts: 24.2 us -> 10.9 us
    mul x12 -> x6, local copies, waits for them, and re-layouts: 15 us -> 0.68 us  [join_softmax(): acc = left[2] * left_factor[..., None] + right[2] * right_factor[..., None]]
where the time goes in v1:
time: 171 us; the launch traced here: 170 us
  blocking collectives  103 us (60%)
  waiting for transfers between devices  30.7 us (18%)
  local copies, waits for them, and re-layouts  10.9 us (6%)
  matrix products  10.8 us (6%)
  starting transfers between devices  9.04 us (5%)
  other arithmetic  4.36 us (3%)
    all_to_all x1, waiting for transfers between devices, sum_at_owner(): lax.all_to_all(pieces, axis, split_axis=0, concat_axis=0, tiled=True)  22.2 us
    all_gather x2, blocking collectives, all_in_one(): both, at, found = (lax.all_gather(jnp.concatenate(lines), axis), 0, {})  22.1 us
    all_to_all x1, blocking collectives, on_device(): all_to_all(jnp.stack(jnp.split(attended, axis_size('grp'), 1), 0), axis_n...  21.9 us
    all_gather x1, blocking collectives, sent_together(): out = lax.all_gather(both, axis, axis=dim, tiled=True)  19.9 us
    all_to_all x1, blocking collectives, on_device(): lax.all_to_all(block_norm, 'grp', split_axis=1, concat_axis=0, tiled=True)  18.6 us
    all_to_all x1, blocking collectives, sum_at_owner_2(): lax.all_to_all(split_up(shard, dim, devices), axis, 0, 0, tiled=True)  11.6 us
    all_to_all x1, blocking collectives, copy_for_each(): lax.all_to_all(jnp.broadcast_to(shard[None], (devices, *shard.shape)), ax...  9.25 us
    all_to_all x1, waiting for transfers between devices, copy_for_each(): lax.all_to_all(jnp.broadcast_to(shard[None], (devices, *shard.shape)), ax...  8.5 us
  transfers between devices with their start and end apart: 2, of which 2 were waited for; matrix products, arithmetic and copies ran while one was open for 0% of the time, Pallas kernels for 0%

profile of v1, /device:TPU:1, one launch (start us, length us, event | category | flops | bytes accessed | tf_op | source)
XLA Modules:
  0.0 170.0 jit_solution(11770587351404022809)
XLA Ops:
  0.0 1.6 copy-done
  1.6 1.2 multiply_reduce_fusion.1
  2.8 0.8 multiply_convert_fusion.1
  3.6 0.2 all_to_all.29
  3.8 18.6 %all_to_all.44 = bf16[14,16,256]{2,0,1:T(8,128)(2,1)S(1)} all-to-all(bf16[14,16,256]{2,0,1:T(8,128)(2,1)S(1)} %copy.44), channel_id=1, replica_groups=mesh['seq_0'=4,'seq_1'=4,'grp'=16] {'grp'}, dimensions={1} | all-to-all | bytes 229376 | tf_op jit(solution)/shard_map/all_to_all | solution.py:179
  22.5 1.1 fusion.65
  23.6 0.2 fusion.66
  23.8 0.2 fusion.67
  24.1 1.0 reshape.558
  25.0 4.2 %all-to-all-start.1 = ((f32[16,14,768]{2,1,0:T(8,128)}), f32[16,14,768]{2,1,0:T(8,128)}, u32[]{:S(2)}, u32[]{:S(2)}) async-start(f32[16,14,768]{2,1,0:T(8,128)} %reshape.558), calls=%async_computation.1 | async-start | bytes 1572864 | tf_op jit(solution)/shard_map/all_to_all | solution.py:19
  29.4 0.1 multiply_cosine_fusion
  29.6 22.2 %all-to-all-done.1 = f32[16,14,768]{2,1,0:T(8,128)} async-done(((f32[16,14,768]{2,1,0:T(8,128)}), f32[16,14,768]{2,1,0:T(8,128)}, u32[]{:S(2)}, u32[]{:S(2)}) %all-to-all-start.1) | async-done | bytes 688160 | tf_op jit(solution)/shard_map/all_to_all | solution.py:19
  51.8 1.2 reduce_sum.64
  53.1 0.1 subtract_convert_fusion.1
  53.2 0.1 pad_maximum_fusion.4
  53.3 0.1 pad_maximum_fusion.5
  53.4 19.9 %all_gather.15 = bf16[42,4096]{1,0:T(8,128)(2,1)S(1)} all-gather(bf16[42,256]{1,0:T(8,128)(2,1)S(1)} %pad_maximum_fusion.3), channel_id=1, replica_groups=mesh['seq_0'=4,'seq_1'=4,'grp'=16] {'seq_0','seq_1'}, dimensions={1}, use_global_device_ids=true | all-gather | bytes 365568 | tf_op jit(solution)/shard_map/all_gather | solution.py:26
  73.5 0.2 convolution_multiply_fusion
  73.7 0.2 copy.85
  73.8 0.1 fusion.45
  74.0 0.1 copy.63
  74.1 3.5 %fusion.63 = (f32[2,7,32]{1,2,0:T(8,128)S(1)}, f32[2,7,32,256]{3,1,2,0:T(8,128)S(1)}) fusion(bf16[2,7,32,128]{3,2,1,0:T(8,128)(2,1)S(1)} %bitcast.262, pred[2,256]{1,0:T(4,128)(4,1)S(1)} %broadcast_compare_fusion, bf16[2,256,4096]{2,1,0:T(8,128)(2,1)} %param.20), kind=kOutput, calls=%fused_computation.162 | convolution fusion | flops 29703744 | bytes 4770048 | tf_op jit(solution)/shard_map/rthd,rphd->rthp/dot_general | solution.py:219
  77.6 0.1 copy.52
  77.7 0.2 fusion.53
  77.9 0.2 copy.54
  78.1 0.3 fusion.23
  78.4 0.2 convolution_bitcast_fusion
  78.6 2.9 %fusion.20 = f32[2,7,32,128]{3,1,2,0:T(8,128)S(1)} fusion(f32[2,7,32,128]{3,1,2,0:T(8,128)S(1)} %convolution_bitcast_fusion, f32[2,7,32,256]{3,1,2,0:T(8,128)S(1)} %get-tuple-element.74, f32[2,7,32]{1,2,0:T(8,128)S(1)} %max.134, pred[2,256]{1,0:T(4,128)(4,1)S(1)} %broadcast_compare_fusion, bf16[2,256,4096]{2,1,0:T(8,128)(2,1)} %param.21), kind=kOutput, calls=%fused_computation.12 | convolution fusion | flops 29761536 | bytes 5114112 | tf_op jit(solution)/shard_map/rthp,rphd->rthd/dot_general | solution.py:231
  81.6 0.1 copy.64
  81.7 0.1 copy.58
  82.0 10.7 %all-gather = f32[1824,128]{1,0:T(8,128)S(1)} all-gather(f32[456,128]{1,0:T(8,128)S(1)} %pad_maximum_fusion.1), channel_id=2, replica_groups=mesh['seq_0'=4,'seq_1'=4,'grp'=16] {'seq_0'}, dimensions={0}, use_global_device_ids=true | all-gather | bytes 1167360 | tf_op jit(solution)/shard_map/all_gather | solution.py:38
  92.8 0.4 fusion.30
  93.2 11.3 %all-gather.1 = f32[1824,128]{1,0:T(8,128)S(1)} all-gather(f32[456,128]{1,0:T(8,128)S(1)} %pad_maximum_fusion.2), channel_id=3, replica_groups=mesh['seq_0'=4,'seq_1'=4,'grp'=16] {'seq_1'}, dimensions={0}, use_global_device_ids=true | all-gather | bytes 1167360 | tf_op jit(solution)/shard_map/all_gather | solution.py:38
  104.6 0.7 fusion.57
  105.4 1.0 squeeze.92
  107.1 0.1 mul.412
  107.3 0.2 copy.81
  107.5 0.1 div.26
  107.6 0.2 copy.83
  107.8 0.1 mul.397
  107.9 0.2 copy.76
  108.1 0.1 mul.400
  108.2 0.2 copy.77
  108.4 0.1 mul.403
  108.6 0.2 copy.78
  108.7 0.1 mul.406
  108.9 0.2 copy.79
  109.0 0.1 mul.409
  109.2 0.2 copy.80
  109.4 0.1 divide_convert_fusion
  109.7 21.9 %all_to_all.45 = bf16[16,14,256]{2,1,0:T(8,128)(2,1)S(1)} all-to-all(bf16[16,14,256]{2,1,0:T(8,128)(2,1)S(1)} %constant_dynamic-update-slice_fusion), channel_id=1, replica_groups=mesh['seq_0'=4,'seq_1'=4,'grp'=16] {'grp'}, dimensions={0} | all-to-all | bytes 229376 | tf_op jit(solution)/shard_map/all_to_all | solution.py:247
  131.6 0.2 convolution_convert_fusion
  131.9 11.6 %all_to_all.46 = bf16[16,14,256]{2,1,0:T(8,128)(2,1)S(1)} all-to-all(bf16[16,14,256]{2,1,0:T(8,128)(2,1)S(1)} %reshape.576), channel_id=1, replica_groups=mesh['seq_0'=4,'seq_1'=4,'grp'=16] {'grp'}, dimensions={0} | all-to-all | bytes 229376 | tf_op jit(solution)/shard_map/all_to_all | solution.py:58
  143.4 0.7 broadcast_in_dim.49
  144.2 4.9 %all-to-all-start.4 = ((f32[16,14,256]{2,1,0:T(8,128)}), f32[16,14,256]{2,1,0:T(8,128)S(1)}, u32[]{:S(2)}, u32[]{:S(2)}) async-start(f32[16,14,256]{2,1,0:T(8,128)} %broadcast_in_dim.49), calls=%async_computation.4 | async-start | bytes 524288 | tf_op jit(solution)/shard_map/all_to_all | solution.py:70
  149.1 8.5 %all-to-all-done.4 = f32[16,14,256]{2,1,0:T(8,128)S(1)} async-done(((f32[16,14,256]{2,1,0:T(8,128)}), f32[16,14,256]{2,1,0:T(8,128)S(1)}, u32[]{:S(2)}, u32[]{:S(2)}) %all-to-all-start.4) | async-done | bytes 229408 | tf_op jit(solution)/shard_map/all_to_all | solution.py:70
  157.6 0.1 copy.59
  157.8 0.1 multiply_reduce_fusion
  158.0 0.1 rsqrt.21
  158.0 0.2 copy.84
  158.2 1.3 fusion.64
  159.5 0.2 exponential_reduce_fusion
  159.7 9.3 %all_to_all.47 = f32[16,2,14]{2,1,0:T(2,128)S(1)} all-to-all(f32[16,2,14]{2,1,0:T(2,128)S(1)} %broadcast_in_dim.50), channel_id=1, replica_groups=mesh['seq_0'=4,'seq_1'=4,'grp'=16] {'seq_0','seq_1'}, dimensions={0} | all-to-all | bytes 3584 | tf_op jit(solution)/shard_map/all_to_all | solution.py:70
  169.4 0.6 copy.62
  (123 shorter events, 2.6 us)
Async XLA Ops:
  0.0 1.6 copy-start
  0.0 23.6 %copy-start.1 = (bf16[256,256]{1,0:T(8,128)(2,1)S(1)}, bf16[256,256]{1,0:T(8,128)(2,1)}, u32[]{:S(2)}) copy-start(bf16[256,256]{1,0:T(8,128)(2,1)} %param.17) | copy-start | bytes 393220
  0.0 23.8 %copy-start.2 = (bf16[256,256]{1,0:T(8,128)(2,1)S(1)}, bf16[256,256]{1,0:T(8,128)(2,1)}, u32[]{:S(2)}) copy-start(bf16[256,256]{1,0:T(8,128)(2,1)} %param.18) | copy-start | bytes 393220
  2.8 26.5 %copy-start.5 = (s32[2]{0:T(128)S(1)}, s32[2]{0:T(128)}, u32[]{:S(2)}) copy-start(s32[2]{0:T(128)} %param.13) | copy-start | bytes 28
  25.0 26.8 %all-to-all-start.1 = ((f32[16,14,768]{2,1,0:T(8,128)}), f32[16,14,768]{2,1,0:T(8,128)}, u32[]{:S(2)}, u32[]{:S(2)}) async-start(f32[16,14,768]{2,1,0:T(8,128)} %reshape.558), calls=%async_computation.1 | async-start | bytes 1572864 | tf_op jit(solution)/shard_map/all_to_all | solution.py:19
  108.2 23.4 %copy-start.3 = (bf16[256,256]{1,0:T(8,128)(2,1)S(1)}, bf16[256,256]{1,0:T(8,128)(2,1)}, u32[]{:S(2)}) copy-start(bf16[256,256]{1,0:T(8,128)(2,1)} %param.19) | copy-start | bytes 393220
  109.3 48.9 %copy-start.4 = (f32[4096]{0:T(1024)S(1)}, f32[4096]{0:T(1024)}, u32[]{:S(2)}) copy-start(f32[4096]{0:T(1024)} %param.22) | copy-start | bytes 49156
  144.2 13.4 %all-to-all-start.4 = ((f32[16,14,256]{2,1,0:T(8,128)}), f32[16,14,256]{2,1,0:T(8,128)S(1)}, u32[]{:S(2)}, u32[]{:S(2)}) async-start(f32[16,14,256]{2,1,0:T(8,128)} %broadcast_in_dim.49), calls=%async_computation.4 | async-start | bytes 524288 | tf_op jit(solution)/shard_map/all_to_all | solution.py:70
